TPU v7x, 128 devices: a whole 4x4x4 slice. The times are simulated.
128 devices in a mesh: tm: 16 (over z, x_hi, core), space: 8 (over x_lo, y).
Axes of the slice: x: 4 (x_hi: 2, x_lo: 2; x = x_hi * 2 + x_lo), y: 4, z: 4, core: 2. Of those that a mesh axis runs over, the one named last changes fastest.
Arguments:
- solution: float32 [512, 384, 384], P('tm', 'space'), may hold values from -6 to 6
- residual: float32 [512, 384, 384], P('tm', 'space'), may hold values from -6 to 6
- direction: float32 [512, 384, 384], P('tm', 'space'), may hold values from -6 to 6
- reaction: float32 [512, 384, 384], P('tm', 'space'), may hold values from 0.1 to 2
- time_bands: float32 [2, 4, 512], replicated, may hold values from -0.25 to 1.1, as said below
- space_bands: float32 [2, 4, 384], replicated, may hold values from -0.25 to 1.1, as said below
- time_basis: float32 [512, 512], replicated, may hold values from -0.25 to 0.25
- space_basis: float32 [384, 384], replicated, may hold values from -0.3125 to 0.3125
- time_eigen: float32 [512], replicated, may hold values from 0.1 to 1
- space_eigen: float32 [384], replicated, may hold values from 0.1 to 1
Outputs:
- new_solution: float32 [512, 384, 384], P('tm', 'space')
- new_residual: float32 [512, 384, 384], P('tm', 'space')
- new_direction: float32 [512, 384, 384], P('tm', 'space')
Inputs may be any that keep to these rules, and one draw needn't show every extreme that they name: `time_bands`: each of the two matrices is symmetric with every diagonal entry larger than the sum of the magnitudes of the other entries of its row. `space_bands`: each of the two matrices is symmetric with every diagonal entry larger than the sum of the magnitudes of the other entries of its row.
All inputs are finite; a program needn't handle non-finite values.
Results may differ from a plain program's by a relative error of at most 0.000051.
Values sent between devices are 32-bit elements; how exact they have to be, the bound alone decides.
A program may use at most 128 MiB of HBM per device.

v0:
```python
import jax
import jax.numpy as jnp
from jax import lax
from jax.sharding import Mesh
from jax.sharding import PartitionSpec as P

TM_SPACE = ("tm_0", "tm_1", "tm_2", "space_0", "space_1")
TM = ("tm_0", "tm_1", "tm_2")
SPACE = ("space_0", "space_1")
highest = lax.Precision.HIGHEST


def extended_2(cells, sides, width):
    for axis, dim in sides:
        count = lax.axis_size(axis)
        ends = count - 1
        head = lax.slice_in_dim(cells, 0, width, axis=dim)
        tail = lax.slice_in_dim(cells, cells.shape[dim] - width, cells.shape[dim], axis=dim)
        cells = jnp.concatenate(
            [
                lax.ppermute(tail, axis, [(i, (i + 1) % count) for i in range(ends)]),
                cells,
                lax.ppermute(head, axis, [((i + 1) % count, i) for i in range(ends)]),
            ],
            axis=dim,
        )
    return cells


def cut_along(shard, dim, count):
    before, after = (shard.shape[:dim], shard.shape[dim + 1 :])
    return jnp.moveaxis(shard.reshape(*before, count, -1, *after), dim, 0)


def joined_along(pieces, dim):
    lengths = list(pieces.shape[1:])
    lengths[dim] *= pieces.shape[0]
    return jnp.moveaxis(pieces, 0, dim).reshape(lengths)


def exchange_in_order(pieces, axes, turns):
    lengths = [lax.axis_size(a) for a in axes]
    pieces = pieces.reshape(*lengths, *pieces.shape[1:])
    for k in turns:
        pieces = lax.all_to_all(pieces, axes[k], split_axis=k, concat_axis=k, tiled=True)
    return pieces.reshape(-1, *pieces.shape[len(axes) :])


def two_step_exchange(shard, groups, turns, split_dim, concat_dim):
    count = lax.axis_size(groups[0]) * lax.axis_size(groups[1])
    pieces = cut_along(shard, split_dim, count)
    return joined_along(exchange_in_order(pieces, groups, turns), concat_dim)


def over_axes(shard, axes):
    for axis in axes:
        shard = lax.psum(shard, axis)
    return shard


def band_apply(extended, band_rows, dimension):
    length = extended.shape[dimension] - 6
    target_shape = [1] * extended.ndim
    target_shape[dimension] = length

    def coefficient(which_row, first_row):
        return lax.slice_in_dim(band_rows[which_row], first_row, first_row + length).reshape(
            target_shape
        )

    def window(first_row):
        return lax.slice_in_dim(extended, first_row, first_row + length, axis=dimension)

    result = coefficient(0, 3) * window(3)
    for offset in (1, 2, 3):
        result = (
            result
            + coefficient(offset, 3) * window(3 + offset)
            + coefficient(offset, 3 - offset) * window(3 - offset)
        )
    return result


def pad_along(values, dimension):
    widths = [(0, 0)] * values.ndim
    widths[dimension] = (3, 3)
    return jnp.pad(values, widths)


def apply_operator(direction, reaction, time_bands, space_bands):
    rows_time = direction.shape[0]
    rows_space = direction.shape[1]
    halo_block = extended_2(direction, ((TM, 0), (SPACE, 1)), 3)
    padded_time = jnp.pad(time_bands, ((0, 0), (0, 0), (3, 3)))
    padded_space = jnp.pad(space_bands, ((0, 0), (0, 0), (3, 3)))
    time_rows = lax.dynamic_slice_in_dim(
        padded_time, lax.axis_index(TM) * rows_time, rows_time + 6, 2
    )
    space_rows = lax.dynamic_slice_in_dim(
        padded_space, lax.axis_index(SPACE) * rows_space, rows_space + 6, 2
    )
    extended = pad_along(halo_block, 2)
    mass_y = band_apply(extended, padded_space[1], 2)
    stiff_y = band_apply(extended, padded_space[0], 2)
    mass_xy = band_apply(mass_y, space_rows[1], 1)
    stiff_x = band_apply(mass_y, space_rows[0], 1)
    stiff_yx = band_apply(stiff_y, space_rows[1], 1)
    temporal = band_apply(mass_xy, time_rows[0], 0) + band_apply(
        stiff_x + stiff_yx, time_rows[1], 0
    )
    return temporal + reaction * direction


def spectrum(time_eigen, space_eigen):
    time_count = lax.axis_size(TM)
    space_count = lax.axis_size(SPACE)
    block_width = space_eigen.shape[0] // (time_count * space_count)
    group_index = lax.axis_index(SPACE) * time_count + lax.axis_index(TM)
    block = lax.dynamic_slice_in_dim(space_eigen, group_index * block_width, block_width)
    return time_eigen[:, None, None] + space_eigen[None, :, None] + block[None, None, :]


def forward_fields(fields, time_basis, space_basis):
    along_y = jnp.einsum("ctxk,ka->ctxa", fields, space_basis, precision=highest)
    spread = lax.all_to_all(along_y, SPACE, split_axis=3, concat_axis=2, tiled=True)
    along_x = jnp.einsum("ctjy,jb->ctby", spread, space_basis, precision=highest)
    joined = lax.all_to_all(along_x, TM, split_axis=3, concat_axis=1, tiled=True)
    return jnp.einsum("cixy,ia->caxy", joined, time_basis, precision=highest)


def inverse_fields(spectral, time_basis, space_basis):
    along_t = jnp.einsum("caxy,ia->cixy", spectral, time_basis, precision=highest)
    parted = two_step_exchange(along_t, (("tm_0", "tm_1"), "tm_2"), (1, 0), 1, 3)
    along_x = jnp.einsum("ctby,jb->ctjy", parted, space_basis, precision=highest)
    blocks = lax.all_to_all(along_x, SPACE, split_axis=2, concat_axis=3, tiled=True)
    return jnp.einsum("ctxa,ka->ctxk", blocks, space_basis, precision=highest)


def per_device(
    solution,
    residual,
    direction,
    reaction,
    time_bands,
    space_bands,
    time_basis,
    space_basis,
    time_eigen,
    space_eigen,
):
    image = apply_operator(direction, reaction, time_bands, space_bands)
    eigen_sum = spectrum(time_eigen, space_eigen)
    both_hat = forward_fields(jnp.stack([residual, image]), time_basis, space_basis)
    first_scaled = both_hat[0] / eigen_sum
    image_scaled = both_hat[1] / eigen_sum
    norm_old, cross_term, image_norm, curvature = (
        over_axes(jnp.sum(both_hat[0] * first_scaled), TM_SPACE),
        over_axes(jnp.sum(both_hat[1] * first_scaled), TM_SPACE),
        over_axes(jnp.sum(both_hat[1] * image_scaled), TM_SPACE),
        over_axes(jnp.sum(direction * image), TM_SPACE),
    )
    step_size = norm_old / curvature
    new_residual = residual - step_size * image
    spectral = first_scaled - step_size * image_scaled
    norm_new = norm_old - 2.0 * step_size * cross_term + step_size * step_size * image_norm
    precond = inverse_fields(spectral[None], time_basis, space_basis)[0]
    new_direction = precond + norm_new / norm_old * direction
    new_solution = solution + step_size * direction
    return (new_solution, new_residual, new_direction)


def solution(mesh):
    finer = Mesh(
        mesh.devices.reshape(4, 2, 2, 2, 4), ("tm_0", "tm_1", "tm_2", "space_0", "space_1")
    )
    in_specs = (
        P(TM, SPACE, None),
        P(TM, SPACE, None),
        P(TM, SPACE, None),
        P(TM, SPACE, None),
        P(),
        P(),
        P(),
        P(),
        P(),
        P(),
    )
    out_specs = (P(TM, SPACE, None), P(TM, SPACE, None), P(TM, SPACE, None))
    return jax.shard_map(
        per_device, mesh=finer, in_specs=in_specs, out_specs=out_specs, check_vma=False
    )
```

profile of v0, /device:TPU:1, one launch (start us, length us, event | category | flops | bytes accessed | tf_op | source)
XLA Modules:
  0.0 526.5 jit_solution(127195260726409566)
XLA Ops:
  1.8 6.0 %collective-permute-start = (f32[3,48,384]{2,1,0:T(8,128)S(1)}, f32[3,48,384]{2,1,0:T(8,128)S(1)}, u32[]{:S(2)}, u32[]{:S(2)}) collective-permute-start(f32[3,48,384]{2,1,0:T(8,128)S(1)} %get-tuple-element.47), channel_id=1, source_target_pairs={{0,8},{8,16},{16,24},{24,32},{32,40},{40,48},{48,56},{56,64},{64,7... | collective-permute-start | bytes 663560 | tf_op jit(solution)/shard_map/ppermute | solution.py:21
  28.8 30.2 %multiply_add_fusion.1 = (f32[38,54,384]{2,1,0:T(8,128)}, f32[38,54,384]{2,1,0:T(8,128)}) fusion(f32[38,54,384]{2,1,0:T(8,128)} %pad_maximum_fusion, f32[384]{0:T(512)S(1)} %get-tuple-element.9, f32[384]{0:T(512)S(1)} %get-tuple-element.15, f32[384]{0:T(512)S(1)} %get-tuple-element.8, f32[384]{0:T(512)S(1)} %get-tuple-element.16, ...), kind=kLoop, calls=%fused_computation.18 | loop fusion | flops 20487168 | bytes 9477120 | tf_op jit(solution)/shard_map/add | solution.py:77
  59.0 12.2 %multiply_add_fusion.2 = f32[38,48,384]{2,1,0:T(8,128)} fusion(f32[38,54,384]{2,1,0:T(8,128)} %get-tuple-element.42, f32[48]{0:T(128)S(1)} %get-tuple-element.70, f32[48]{0:T(128)S(1)} %get-tuple-element.71, f32[48]{0:T(128)S(1)} %get-tuple-element.72, f32[48]{0:T(128)S(1)} %get-tuple-element.73, f32[48]{0:T(128)S(1)} %get-tuple-element.75, ...), kind=kLoop, calls=%fused_computation.33 | loop fusion | flops 9105408 | bytes 22414656 | tf_op jit(solution)/shard_map/add | solution.py:77
  77.1 16.6 %multiply_reduce_fusion = (f32[]{:T(128)}, f32[32,48,384]{2,1,0:T(8,128)S(1)}) fusion(f32[32,48,384]{2,1,0:T(8,128)} %param.12, f32[32,48,384]{2,1,0:T(8,128)} %param.13, f32[38,48,384]{2,1,0:T(8,128)} %fusion.5, f32[32]{0:T(128)S(1)} %get-tuple-element.54, f32[32]{0:T(128)S(1)} %get-tuple-element.55, f32[32]{0:T(128)S(1)} %get-tuple-element.53, ...), kind=kLoop, calls=%fused_computation.75 | loop fusion | flops 18284544 | bytes 40109828 | tf_op jit(solution)/shard_map/reduce_sum | solution.py:160
  95.1 10.6 %fusion = f32[2,32,48,384]{3,2,1,0:T(8,128)} fusion(f32[1,32,48,384]{3,2,1,0:T(8,128)S(1)} %bitcast.155, f32[1,32,48,384]{3,2,1,0:T(8,128)S(1)} %bitcast.157, f32[384,384]{1,0:T(8,128)S(1)} %copy-done.7), kind=kOutput, calls=%fused_computation.8 | convolution fusion | flops 5436997632 | bytes 10027008 | tf_op jit(solution)/shard_map/ctxk,ka->ctxa/dot_general | solution.py:124
  105.7 12.0 %copy.26 = f32[2,32,48,384]{2,1,0,3:T(8,128)} copy(f32[2,32,48,384]{3,2,1,0:T(8,128)} %fusion) | data formatting | bytes 9437184 | tf_op jit(solution)/shard_map/ctxk,ka->ctxa/dot_general | solution.py:124
  117.8 14.4 %reshape.301 = f32[8,1,147456]{2,1,0:T(1,128)} reshape(f32[384,2,32,48]{3,2,1,0:T(8,128)} %bitcast.151) | data formatting | bytes 9437184
  132.2 57.9 %all_to_all.61 = f32[8,1,147456]{2,1,0:T(1,128)} all-to-all(f32[8,1,147456]{2,1,0:T(1,128)} %reshape.301), channel_id=1, replica_groups=mesh['tm_0'=4,'tm_1'=2,'tm_2'=2,'space_0'=2,'space_1'=4] {'space_0','spa..., dimensions={0} | all-to-all | bytes 9437184 | tf_op jit(solution)/shard_map/all_to_all | solution.py:125
  190.5 15.9 %reduce.28 = f32[8,147456]{1,0:T(8,128)} reduce(f32[8,1,147456]{2,1,0:T(1,128)} %all_to_all.61, f32[]{:T(128)} %broadcast.59), dimensions={1}, to_apply=%all_to_all.43.reduce_sub_computation | reduce | bytes 9437188 | tf_op jit(solution)/shard_map/all_to_all | solution.py:125
  206.4 11.9 %reshape.302 = f32[384,2,32,48]{3,2,1,0:T(8,128)} reshape(f32[8,147456]{1,0:T(8,128)} %reduce.28) | data formatting | bytes 9437184
  218.4 16.7 %copy.52 = f32[2,32,48,8,48]{2,3,4,1,0:T(8,128)} copy(f32[2,32,48,8,48]{2,1,0,4,3:T(8,128)} %bitcast.149) | data formatting | bytes 9437184 | tf_op jit(solution)/shard_map/all_to_all | solution.py:125
  235.1 10.7 %all_to_all.46 = f32[2,32,384,48]{2,3,1,0:T(8,128)} reshape(f32[2,32,8,48,48]{3,2,4,1,0:T(8,128)} %bitcast.150) | data formatting | bytes 9437184 | tf_op jit(solution)/shard_map/all_to_all | solution.py:125
  245.8 11.8 %convolution_bitcast_fusion = f32[2,32,384,48]{2,3,1,0:T(8,128)S(1)} fusion(f32[2,32,384,48]{2,3,1,0:T(8,128)} %all_to_all.46, f32[384,384]{1,0:T(8,128)S(1)} %copy-done.7), kind=kOutput, calls=%fused_computation.77 | convolution fusion | flops 5435817984 | bytes 10027008 | tf_op jit(solution)/shard_map/ctjy,jb->ctby/dot_general | solution.py:126
  261.2 13.3 %all-to-all-start.1 = ((f32[2,32,384,48]{2,1,0,3:T(8,128)}), f32[2,32,384,48]{2,1,0,3:T(8,128)}, u32[]{:S(2)}, u32[]{:S(2)}) async-start(f32[2,32,384,48]{2,1,0,3:T(8,128)} %copy.28), calls=%async_computation.1 | async-start | bytes 9437184 | tf_op jit(solution)/shard_map/all_to_all | solution.py:127
  274.7 56.2 %all-to-all-done.1 = f32[2,32,384,48]{2,1,0,3:T(8,128)} async-done(((f32[2,32,384,48]{2,1,0,3:T(8,128)}), f32[2,32,384,48]{2,1,0,3:T(8,128)}, u32[]{:S(2)}, u32[]{:S(2)}) %all-to-all-start.1) | async-done | bytes 4718624 | tf_op jit(solution)/shard_map/all_to_all | solution.py:127
  333.7 8.0 %convolution_bitcast_fusion.1 = f32[2,512,384,3]{1,2,3,0:T(8,128)S(1)} fusion(f32[2,512,384,3]{2,1,3,0:T(8,128)S(1)} %bitcast.156, f32[512,512]{1,0:T(8,128)S(1)} %copy-done), kind=kOutput, calls=%fused_computation.78 | convolution fusion | flops 7247757312 | bytes 10485760 | tf_op jit(solution)/shard_map/cixy,ia->caxy/dot_general | solution.py:128
  346.0 7.9 %all-reduce.4 = (f32[]{:T(128)}, f32[]{:T(128)}, f32[]{:T(128)}, f32[]{:T(128)}) all-reduce(f32[]{:T(128)} %get-tuple-element.5, f32[]{:T(128)} %get-tuple-element.40, f32[]{:T(128)} %get-tuple-element.4, f32[]{:T(128)} %get-tuple-element.3), channel_id=1, replica_groups=mesh['tm_0'=4,'tm_1'=2,'tm_2'=2,'space_0'=2,'space_1'=4] {'tm_0'}, use_global_device_ids=true, to_apply=%region_1.2 | all-reduce | flops 4 | bytes 32 | tf_op jit(solution)/shard_map/psum | solution.py:57
  353.9 6.0 %all-reduce.7 = (f32[]{:T(128)}, f32[]{:T(128)}, f32[]{:T(128)}, f32[]{:T(128)}) all-reduce(f32[]{:T(128)} %get-tuple-element.24, f32[]{:T(128)} %get-tuple-element.25, f32[]{:T(128)} %get-tuple-element.26, f32[]{:T(128)} %get-tuple-element.27), channel_id=1, replica_groups=mesh['tm_0'=4,'tm_1'=2,'tm_2'=2,'space_0'=2,'space_1'=4] {'tm_1'}, use_global_device_ids=true, to_apply=%region_2.3 | all-reduce | flops 4 | bytes 32 | tf_op jit(solution)/shard_map/psum | solution.py:57
  359.9 7.0 %all-reduce.6 = (f32[]{:T(128)}, f32[]{:T(128)}, f32[]{:T(128)}, f32[]{:T(128)}) all-reduce(f32[]{:T(128)} %get-tuple-element.36, f32[]{:T(128)} %get-tuple-element.37, f32[]{:T(128)} %get-tuple-element.38, f32[]{:T(128)} %get-tuple-element.39), channel_id=1, replica_groups=mesh['tm_0'=4,'tm_1'=2,'tm_2'=2,'space_0'=2,'space_1'=4] {'tm_2'}, use_global_device_ids=true, to_apply=%region_3.4 | all-reduce | flops 4 | bytes 32 | tf_op jit(solution)/shard_map/psum | solution.py:57
  371.4 7.6 %all-reduce.3 = (f32[]{:T(128)}, f32[]{:T(128)}, f32[]{:T(128)}, f32[]{:T(128)}) all-reduce(f32[]{:T(128)} %get-tuple-element.28, f32[]{:T(128)} %get-tuple-element.29, f32[]{:T(128)} %get-tuple-element.30, f32[]{:T(128)} %get-tuple-element.31), channel_id=1, replica_groups=mesh['tm_0'=4,'tm_1'=2,'tm_2'=2,'space_0'=2,'space_1'=4] {'space_1'}, use_global_device_ids=true, to_apply=%region_5.6 | all-reduce | flops 4 | bytes 32 | tf_op jit(solution)/shard_map/psum | solution.py:57
  380.3 7.2 %fusion.38 = f32[8,2,1,32,384,3]{4,3,1,0,5,2:T(8,128)S(1)} fusion(f32[8,2,32,512,1]{3,2,1,0,4:T(8,128)S(1)} %bitcast.148, f32[2,512,384,3]{1,2,3,0:T(8,128)} %copy-done.5, f32[]{:T(128)S(6)} %div.19, f32[3]{0:T(128)S(1)} %dynamic_slice.11, f32[512,384]{0,1:T(8,128)S(1)} %broadcast_add_fusion), kind=kOutput, calls=%fused_computation.81 | convolution fusion | flops 3626827776 | bytes 8912912 | tf_op jit(solution)/shard_map/caxy,ia->cixy/dot_general | solution.py:132
  387.7 8.8 %all_to_all.62 = f32[8,2,1,32,384,3]{4,3,0,5,2,1:T(8,128)S(1)} all-to-all(f32[8,2,1,32,384,3]{4,3,0,5,2,1:T(8,128)S(1)} %copy.33), channel_id=1, replica_groups=mesh['tm_0'=4,'tm_1'=2,'tm_2'=2,'space_0'=2,'space_1'=4] {'tm_2'}, dimensions={1} | all-to-all | bytes 4718592 | tf_op jit(solution)/shard_map/all_to_all | solution.py:45
  396.7 33.4 %all_to_all.63 = f32[8,2,1,32,384,3]{4,3,1,5,2,0:T(8,128)S(1)} all-to-all(f32[8,2,1,32,384,3]{4,3,1,5,2,0:T(8,128)S(1)} %copy.34), channel_id=1, replica_groups=mesh['tm_0'=4,'tm_1'=2,'tm_2'=2,'space_0'=2,'space_1'=4] {'tm_0','tm_1'}, dimensions={0} | all-to-all | bytes 4718592 | tf_op jit(solution)/shard_map/all_to_all | solution.py:45
  430.3 7.2 %fusion.41 = f32[1,32,384,48]{2,3,1,0:T(8,128)} fusion(f32[32,384,48]{1,0,2:T(8,128)S(1)} %bitcast.158, f32[384,384]{1,0:T(8,128)S(1)} %copy-done.7), kind=kOutput, calls=%fused_computation.82 | convolution fusion | flops 2717908992 | bytes 5308416 | tf_op jit(solution)/shard_map/ctby,jb->ctjy/dot_general | solution.py:134
  437.5 7.2 %copy.37 = f32[1,32,384,48]{3,1,0,2:T(8,128)} copy(f32[1,32,384,48]{2,3,1,0:T(8,128)} %fusion.41) | data formatting | bytes 4718592 | tf_op jit(solution)/shard_map/ctby,jb->ctjy/transpose | solution.py:134
  444.7 9.5 %reshape.303 = f32[8,1,73728]{2,1,0:T(1,128)} reshape(f32[384,1,32,48]{3,2,1,0:T(8,128)} %bitcast.154) | data formatting | bytes 4718592
  467.2 20.5 %all-to-all-done.4 = f32[8,1,73728]{2,1,0:T(1,128)} async-done(((f32[8,1,73728]{2,1,0:T(1,128)}), f32[8,1,73728]{2,1,0:T(1,128)}, u32[]{:S(2)}, u32[]{:S(2)}) %all-to-all-start.4) | async-done | bytes 2359328 | tf_op jit(solution)/shard_map/all_to_all | solution.py:135
  487.7 9.3 %reduce.29 = f32[8,73728]{1,0:T(8,128)} reduce(f32[8,1,73728]{2,1,0:T(1,128)} %all-to-all-done.4, f32[]{:T(128)} %broadcast.59), dimensions={1}, to_apply=%all_to_all.53.reduce_sub_computation | reduce | bytes 4718596 | tf_op jit(solution)/shard_map/all_to_all | solution.py:135
  497.0 6.9 %reshape.304 = f32[384,1,32,48]{3,2,1,0:T(8,128)} reshape(f32[8,73728]{1,0:T(8,128)} %reduce.29) | data formatting | bytes 4718592
  503.9 9.3 %copy.53 = f32[1,32,8,48,48]{4,2,3,1,0:T(8,128)} copy(f32[1,32,8,48,48]{4,1,3,2,0:T(8,128)} %bitcast.152) | data formatting | bytes 4718592 | tf_op jit(solution)/shard_map/all_to_all | solution.py:135
  513.2 5.9 %reshape.281 = f32[32,48,384]{2,1,0:T(8,128)} reshape(f32[1,32,48,8,48]{4,3,2,1,0:T(8,128)} %bitcast.153) | data formatting | bytes 4718592 | tf_op jit(solution)/shard_map/reshape.193
  519.1 7.2 %multiply_add_fusion.3 = f32[32,48,384]{2,1,0:T(8,128)} fusion(f32[32,48,384]{2,1,0:T(8,128)S(1)} %copy-done.3, f32[32,48,384]{2,1,0:T(8,128)} %reshape.281, f32[]{:T(128)S(6)} %div.23, f32[384,384]{1,0:T(8,128)} %param.17), kind=kOutput, calls=%fused_computation.72 | convolution fusion | flops 2719088640 | bytes 7667716 | tf_op jit(solution)/shard_map/ctxa,ka->ctxk/dot_general | solution.py:136
  (55 shorter events, 56.3 us)
Async XLA Ops:
  0.6 333.0 %copy-start = (f32[512,512]{1,0:T(8,128)S(1)}, f32[512,512]{1,0:T(8,128)}, u32[]{:S(2)}) copy-start(f32[512,512]{1,0:T(8,128)} %param.16) | copy-start | bytes 3145732
  1.8 11.0 %collective-permute-start = (f32[3,48,384]{2,1,0:T(8,128)S(1)}, f32[3,48,384]{2,1,0:T(8,128)S(1)}, u32[]{:S(2)}, u32[]{:S(2)}) collective-permute-start(f32[3,48,384]{2,1,0:T(8,128)S(1)} %get-tuple-element.47), channel_id=1, source_target_pairs={{0,8},{8,16},{16,24},{24,32},{32,40},{40,48},{48,56},{56,64},{64,7... | collective-permute-start | bytes 663560 | tf_op jit(solution)/shard_map/ppermute | solution.py:21
  7.8 8.8 %collective-permute-start.1 = (f32[3,48,384]{2,1,0:T(8,128)S(1)}, f32[3,48,384]{2,1,0:T(8,128)S(1)}, u32[]{:S(2)}, u32[]{:S(2)}) collective-permute-start(f32[3,48,384]{2,1,0:T(8,128)S(1)} %get-tuple-element.46), channel_id=1, source_target_pairs={{8,0},{16,8},{24,16},{32,24},{40,32},{48,40},{56,48},{64,56},{72,6... | collective-permute-start | bytes 663560 | tf_op jit(solution)/shard_map/ppermute | solution.py:23
  12.8 8.4 %copy-start.9 = (f32[2,4,512]{2,1,0:T(4,128)S(1)}, f32[2,4,512]{2,1,0:T(4,128)}, u32[]{:S(2)}) copy-start(f32[2,4,512]{2,1,0:T(4,128)} %param.14) | copy-start | bytes 49156
  12.8 8.5 %copy-start.8 = (f32[2,4,384]{2,1,0:T(4,128)S(1)}, f32[2,4,384]{2,1,0:T(4,128)}, u32[]{:S(2)}) copy-start(f32[2,4,384]{2,1,0:T(4,128)} %param.15) | copy-start | bytes 36868
  16.7 6.2 %collective-permute-start.2 = (f32[38,3,384]{2,1,0:T(4,128)S(1)}, f32[38,3,384]{2,1,0:T(4,128)S(1)}, u32[]{:S(2)}, u32[]{:S(2)}) collective-permute-start(f32[38,3,384]{2,1,0:T(4,128)S(1)} %get-tuple-element.44), channel_id=1, source_target_pairs={{0,1},{1,2},{2,3},{3,4},{4,5},{5,6},{6,7},{8,9},{9,10},{10,11},{11... | collective-permute-start | bytes 525320 | tf_op jit(solution)/shard_map/ppermute | solution.py:21
  19.9 6.8 %collective-permute-start.3 = (f32[38,3,384]{2,1,0:T(4,128)S(1)}, f32[38,3,384]{2,1,0:T(4,128)S(1)}, u32[]{:S(2)}, u32[]{:S(2)}) collective-permute-start(f32[38,3,384]{2,1,0:T(4,128)S(1)} %get-tuple-element.45), channel_id=1, source_target_pairs={{1,0},{2,1},{3,2},{4,3},{5,4},{6,5},{7,6},{9,8},{10,9},{11,10},{12... | collective-permute-start | bytes 525320 | tf_op jit(solution)/shard_map/ppermute | solution.py:23
  59.0 12.2 %copy-start.1 = (f32[38,54,384]{2,1,0:T(8,128)S(1)}, f32[38,54,384]{2,1,0:T(8,128)}, u32[]{:S(2)}) copy-start(f32[38,54,384]{2,1,0:T(8,128)} %get-tuple-element.42) | copy-start | bytes 9455620
  59.0 12.2 %copy-start.2 = (f32[38,54,384]{2,1,0:T(8,128)S(1)}, f32[38,54,384]{2,1,0:T(8,128)}, u32[]{:S(2)}) copy-start(f32[38,54,384]{2,1,0:T(8,128)} %get-tuple-element.43) | copy-start | bytes 9455620
  77.1 18.0 %copy-start.6 = (f32[32,48,384]{2,1,0:T(8,128)S(1)}, f32[32,48,384]{2,1,0:T(8,128)}, u32[]{:S(2)}) copy-start(f32[32,48,384]{2,1,0:T(8,128)} %param.11) | copy-start | bytes 7077892
  77.1 18.0 %copy-start.7 = (f32[384,384]{1,0:T(8,128)S(1)}, f32[384,384]{1,0:T(8,128)}, u32[]{:S(2)}) copy-start(f32[384,384]{1,0:T(8,128)} %param.17) | copy-start | bytes 1769476
  93.7 1.4 copy-start.4
  261.2 13.3 %copy-start.10 = (f32[384]{0:T(512)S(1)}, f32[384]{0:T(512)}, u32[]{:S(2)}) copy-start(f32[384]{0:T(512)} %param.19) | copy-start | bytes 4612
  261.2 13.4 %copy-start.11 = (f32[512]{0:T(512)S(1)}, f32[512]{0:T(512)}, u32[]{:S(2)}) copy-start(f32[512]{0:T(512)} %param.18) | copy-start | bytes 6148
  261.2 69.7 %all-to-all-start.1 = ((f32[2,32,384,48]{2,1,0,3:T(8,128)}), f32[2,32,384,48]{2,1,0,3:T(8,128)}, u32[]{:S(2)}, u32[]{:S(2)}) async-start(f32[2,32,384,48]{2,1,0,3:T(8,128)} %copy.28), calls=%async_computation.1 | async-start | bytes 9437184 | tf_op jit(solution)/shard_map/all_to_all | solution.py:127
  341.7 2.1 copy-start.5
  454.2 7.2 %copy-start.3 = (f32[32,48,384]{2,1,0:T(8,128)S(1)}, f32[32,48,384]{2,1,0:T(8,128)}, u32[]{:S(2)}) copy-start(f32[32,48,384]{2,1,0:T(8,128)} %param.12) | copy-start | bytes 7077892
  454.2 33.5 %all-to-all-start.4 = ((f32[8,1,73728]{2,1,0:T(1,128)}), f32[8,1,73728]{2,1,0:T(1,128)}, u32[]{:S(2)}, u32[]{:S(2)}) async-start(f32[8,1,73728]{2,1,0:T(1,128)} %reshape.303), calls=%async_computation.4 | async-start | bytes 4718592 | tf_op jit(solution)/shard_map/all_to_all | solution.py:135
where the time goes:
time: 537 us; the launch traced here: 526 us
  blocking collectives  133 us (25%)
  local copies, waits for them, and re-layouts  122 us (23%)
  other arithmetic  100 us (19%)
  waiting for transfers between devices  83.9 us (16%)
  matrix products  52 us (10%)
  starting transfers between devices  30.4 us (6%)
    all_to_all x1, blocking collectives, forward_fields(): lax.all_to_all(along_y, SPACE, split_axis=3, concat_axis=2, tiled=True)  57.9 us
    all_to_all x1, waiting for transfers between devices, forward_fields(): lax.all_to_all(along_x, TM, split_axis=3, concat_axis=1, tiled=True)  56.2 us
    unnamed x30, local copies, waits for them, and re-layouts  48.1 us
    add x2, other arithmetic, band_apply(): result + coefficient(offset, 3) * window(3 + offset)  42.4 us
    all_to_all x2, blocking collectives, exchange_in_order(): lax.all_to_all(pieces, axes[k], split_axis=k, concat_axis=k, tiled=True)  42.2 us
    psum x5, blocking collectives, over_axes(): shard = lax.psum(shard, axis)  33 us
    all_to_all x3, local copies, waits for them, and re-layouts, forward_fields(): lax.all_to_all(along_y, SPACE, split_axis=3, concat_axis=2, tiled=True)  27.9 us
    all_to_all x1, waiting for transfers between devices, inverse_fields(): lax.all_to_all(along_x, SPACE, split_axis=2, concat_axis=3, tiled=True)  20.5 us
  transfers between devices with their start and end apart: 6, of which 5 were waited for; matrix products, arithmetic and copies ran while one was open for 2% of the time, Pallas kernels for 0%

commit v1 on v0

--- a/solution.py
+++ b/solution.py
@@ -54,7 +54,8 @@
 
 def over_axes(shard, axes):
     for axis in axes:
-        shard = lax.psum(shard, axis)
+        mark_the_rings = lambda x_part, ax_name: jnp.sum(lax.all_gather(x_part, ax_name), 0)
+        shard = mark_the_rings(shard, axis)
     return shard
 
 

time: 537 us -> 573 us (1.067)
  local copies, waits for them, and re-layouts: 122 us -> 153 us
  other arithmetic: 100 us -> 112 us
    psum x5 -> x0, blocking collectives: 33 us -> none  [over_axes(): shard = lax.psum(shard, axis)]
    unnamed x30 -> x85, local copies, waits for them, and re-layouts: 48.1 us -> 78.9 us
    unnamed x0 -> x5, blocking collectives: none -> 29.1 us
    reduce_sum x0 -> x20, other arithmetic: none -> 11.9 us  [over_axes(): jnp.sum(lax.all_gather(x_part, ax_name), 0)]
  transfers between devices with their start and end apart: 6 -> 6, of which waited for: 5 -> 5; matrix products, arithmetic and copies ran while one was open for 2% -> 3% of each run, Pallas kernels for 0% -> 0%
where the time goes in v1:
time: 573 us; the launch traced here: 562 us
  local copies, waits for them, and re-layouts  153 us (27%)
  blocking collectives  130 us (23%)
  other arithmetic  112 us (20%)
  waiting for transfers between devices  80.5 us (14%)
  matrix products  52 us (9%)
  starting transfers between devices  30.1 us (5%)
    unnamed x85, local copies, waits for them, and re-layouts  78.9 us
    all_to_all x1, blocking collectives, forward_fields(): lax.all_to_all(along_y, SPACE, split_axis=3, concat_axis=2, tiled=True)  57.9 us
    all_to_all x1, waiting for transfers between devices, forward_fields(): lax.all_to_all(along_x, TM, split_axis=3, concat_axis=1, tiled=True)  54.1 us
    all_to_all x2, blocking collectives, exchange_in_order(): lax.all_to_all(pieces, axes[k], split_axis=k, concat_axis=k, tiled=True)  42.6 us
    add x2, other arithmetic, band_apply(): result + coefficient(offset, 3) * window(3 + offset)  42.4 us
    unnamed x5, blocking collectives  29.1 us
    all_to_all x3, local copies, waits for them, and re-layouts, forward_fields(): lax.all_to_all(along_y, SPACE, split_axis=3, concat_axis=2, tiled=True)  27.9 us
    all_to_all x1, waiting for transfers between devices, inverse_fields(): lax.all_to_all(along_x, SPACE, split_axis=2, concat_axis=3, tiled=True)  19.1 us
  transfers between devices with their start and end apart: 6, of which 5 were waited for; matrix products, arithmetic and copies ran while one was open for 3% of the time, Pallas kernels for 0%

profile of v1, /device:TPU:1, one launch (start us, length us, event | category | flops | bytes accessed | tf_op | source)
XLA Modules:
  0.0 562.2 jit_solution(1704680860621568538)
XLA Ops:
  1.8 6.0 %collective-permute-start = (f32[3,48,384]{2,1,0:T(8,128)S(1)}, f32[3,48,384]{2,1,0:T(8,128)S(1)}, u32[]{:S(2)}, u32[]{:S(2)}) collective-permute-start(f32[3,48,384]{2,1,0:T(8,128)S(1)} %get-tuple-element.47), channel_id=1, source_target_pairs={{0,8},{8,16},{16,24},{24,32},{32,40},{40,48},{48,56},{56,64},{64,7... | collective-permute-start | bytes 663560 | tf_op jit(solution)/shard_map/ppermute | solution.py:21
  28.8 30.2 %multiply_add_fusion.1 = (f32[38,54,384]{2,1,0:T(8,128)}, f32[38,54,384]{2,1,0:T(8,128)}) fusion(f32[38,54,384]{2,1,0:T(8,128)} %pad_maximum_fusion, f32[384]{0:T(512)S(1)} %get-tuple-element.9, f32[384]{0:T(512)S(1)} %get-tuple-element.15, f32[384]{0:T(512)S(1)} %get-tuple-element.8, f32[384]{0:T(512)S(1)} %get-tuple-element.16, ...), kind=kLoop, calls=%fused_computation.18 | loop fusion | flops 20487168 | bytes 9477120 | tf_op jit(solution)/shard_map/add | solution.py:78
  59.0 12.2 %multiply_add_fusion.2 = f32[38,48,384]{2,1,0:T(8,128)} fusion(f32[38,54,384]{2,1,0:T(8,128)} %get-tuple-element.42, f32[48]{0:T(128)S(1)} %get-tuple-element.70, f32[48]{0:T(128)S(1)} %get-tuple-element.71, f32[48]{0:T(128)S(1)} %get-tuple-element.72, f32[48]{0:T(128)S(1)} %get-tuple-element.73, f32[48]{0:T(128)S(1)} %get-tuple-element.75, ...), kind=kLoop, calls=%fused_computation.33 | loop fusion | flops 9105408 | bytes 22414656 | tf_op jit(solution)/shard_map/add | solution.py:78
  71.2 5.8 %fusion.5 = f32[38,48,384]{2,1,0:T(8,128)} fusion(f32[38,54,384]{2,1,0:T(8,128)S(1)} %copy-done.2, f32[38,54,384]{2,1,0:T(8,128)S(1)} %copy-done.1, f32[48]{0:T(128)S(1)} %get-tuple-element.64, f32[48]{0:T(128)S(1)} %get-tuple-element.65, f32[48]{0:T(128)S(1)} %get-tuple-element.63, f32[48]{0:T(128)S(1)} %get-tuple-element.66, f32[48]{0:T(128)S(1)} %get-tuple-element.68, ...), kind=kLoop, calls=%fused_computation.21 | loop fusion | flops 18911232 | bytes 42027648 | tf_op jit(solution)/shard_map/add | solution.py:110
  77.1 16.6 %multiply_reduce_fusion = (f32[]{:T(128)}, f32[32,48,384]{2,1,0:T(8,128)S(1)}) fusion(f32[32,48,384]{2,1,0:T(8,128)} %param.12, f32[32,48,384]{2,1,0:T(8,128)} %param.13, f32[38,48,384]{2,1,0:T(8,128)} %fusion.5, f32[32]{0:T(128)S(1)} %get-tuple-element.54, f32[32]{0:T(128)S(1)} %get-tuple-element.55, f32[32]{0:T(128)S(1)} %get-tuple-element.53, ...), kind=kLoop, calls=%fused_computation.75 | loop fusion | flops 18284544 | bytes 40109828 | tf_op jit(solution)/shard_map/reduce_sum | solution.py:161
  95.1 10.6 %fusion = f32[2,32,48,384]{3,2,1,0:T(8,128)} fusion(f32[1,32,48,384]{3,2,1,0:T(8,128)S(1)} %bitcast.180, f32[1,32,48,384]{3,2,1,0:T(8,128)S(1)} %bitcast.182, f32[384,384]{1,0:T(8,128)S(1)} %copy-done.7), kind=kOutput, calls=%fused_computation.8 | convolution fusion | flops 5436997632 | bytes 10027008 | tf_op jit(solution)/shard_map/ctxk,ka->ctxa/dot_general | solution.py:125
  105.7 12.0 %copy.26 = f32[2,32,48,384]{2,1,0,3:T(8,128)} copy(f32[2,32,48,384]{3,2,1,0:T(8,128)} %fusion) | data formatting | bytes 9437184 | tf_op jit(solution)/shard_map/ctxk,ka->ctxa/dot_general | solution.py:125
  117.8 14.4 %reshape.401 = f32[8,1,147456]{2,1,0:T(1,128)} reshape(f32[384,2,32,48]{3,2,1,0:T(8,128)} %bitcast.176) | data formatting | bytes 9437184
  132.2 57.9 %all_to_all.61 = f32[8,1,147456]{2,1,0:T(1,128)} all-to-all(f32[8,1,147456]{2,1,0:T(1,128)} %reshape.401), channel_id=1, replica_groups=mesh['tm_0'=4,'tm_1'=2,'tm_2'=2,'space_0'=2,'space_1'=4] {'space_0','spa..., dimensions={0} | all-to-all | bytes 9437184 | tf_op jit(solution)/shard_map/all_to_all | solution.py:126
  190.6 15.9 %reduce.48 = f32[8,147456]{1,0:T(8,128)} reduce(f32[8,1,147456]{2,1,0:T(1,128)} %all_to_all.61, f32[]{:T(128)} %broadcast.79), dimensions={1}, to_apply=%all_to_all.43.reduce_sub_computation | reduce | bytes 9437188 | tf_op jit(solution)/shard_map/all_to_all | solution.py:126
  206.4 11.9 %reshape.402 = f32[384,2,32,48]{3,2,1,0:T(8,128)} reshape(f32[8,147456]{1,0:T(8,128)} %reduce.48) | data formatting | bytes 9437184
  218.4 16.7 %copy.52 = f32[2,32,48,8,48]{2,3,4,1,0:T(8,128)} copy(f32[2,32,48,8,48]{2,1,0,4,3:T(8,128)} %bitcast.174) | data formatting | bytes 9437184 | tf_op jit(solution)/shard_map/all_to_all | solution.py:126
  235.1 10.7 %all_to_all.46 = f32[2,32,384,48]{2,3,1,0:T(8,128)} reshape(f32[2,32,8,48,48]{3,2,4,1,0:T(8,128)} %bitcast.175) | data formatting | bytes 9437184 | tf_op jit(solution)/shard_map/all_to_all | solution.py:126
  245.8 11.8 %convolution_bitcast_fusion = f32[2,32,384,48]{2,3,1,0:T(8,128)S(1)} fusion(f32[2,32,384,48]{2,3,1,0:T(8,128)} %all_to_all.46, f32[384,384]{1,0:T(8,128)S(1)} %copy-done.7), kind=kOutput, calls=%fused_computation.77 | convolution fusion | flops 5435817984 | bytes 10027008 | tf_op jit(solution)/shard_map/ctjy,jb->ctby/dot_general | solution.py:127
  261.2 12.9 %all-to-all-start.1 = ((f32[2,32,384,48]{2,1,0,3:T(8,128)}), f32[2,32,384,48]{2,1,0,3:T(8,128)}, u32[]{:S(2)}, u32[]{:S(2)}) async-start(f32[2,32,384,48]{2,1,0,3:T(8,128)} %copy.28), calls=%async_computation.1 | async-start | bytes 9437184 | tf_op jit(solution)/shard_map/all_to_all | solution.py:128
  276.5 54.1 %all-to-all-done.1 = f32[2,32,384,48]{2,1,0,3:T(8,128)} async-done(((f32[2,32,384,48]{2,1,0,3:T(8,128)}), f32[2,32,384,48]{2,1,0,3:T(8,128)}, u32[]{:S(2)}, u32[]{:S(2)}) %all-to-all-start.1) | async-done | bytes 4718624 | tf_op jit(solution)/shard_map/all_to_all | solution.py:128
  333.5 8.0 %convolution_bitcast_fusion.1 = f32[2,512,384,3]{1,2,3,0:T(8,128)S(1)} fusion(f32[2,512,384,3]{2,1,3,0:T(8,128)S(1)} %bitcast.181, f32[512,512]{1,0:T(8,128)S(1)} %copy-done), kind=kOutput, calls=%fused_computation.78 | convolution fusion | flops 7247757312 | bytes 10485760 | tf_op jit(solution)/shard_map/cixy,ia->caxy/dot_general | solution.py:129
  350.5 7.2 %all-reduce.24 = (f32[4]{0:T(128)S(1)}, f32[4]{0:T(128)S(1)}, f32[4]{0:T(128)S(1)}, f32[4]{0:T(128)S(1)}) all-reduce(f32[4]{0:T(128)S(1)} %dynamic-update-slice, f32[4]{0:T(128)S(1)} %dynamic-update-slice.5, f32[4]{0:T(128)S(1)} %dynamic-update-slice.10, ...), channel_id=1, replica_groups=mesh['tm_0'=4,'tm_1'=2,'tm_2'=2,'space_0'=2,'space_1'=4] {'tm_0'}, use_global_device_ids=true, to_apply=%add.3 | all-reduce | flops 16 | bytes 128
  380.1 6.3 %all-reduce.26 = (f32[2]{0:T(128)S(1)}, f32[2]{0:T(128)S(1)}, f32[2]{0:T(128)S(1)}, f32[2]{0:T(128)S(1)}) all-reduce(f32[2]{0:T(128)S(1)} %dynamic-update-slice.2, f32[2]{0:T(128)S(1)} %dynamic-update-slice.7, f32[2]{0:T(128)S(1)} %dynamic-update-slice.12, ...), channel_id=1, replica_groups=mesh['tm_0'=4,'tm_1'=2,'tm_2'=2,'space_0'=2,'space_1'=4] {'tm_2'}, use_global_device_ids=true, to_apply=%add.5 | all-reduce | flops 8 | bytes 64
  406.5 6.6 %all-reduce.23 = (f32[4]{0:T(128)S(1)}, f32[4]{0:T(128)S(1)}, f32[4]{0:T(128)S(1)}, f32[4]{0:T(128)S(1)}) all-reduce(f32[4]{0:T(128)S(1)} %dynamic-update-slice.4, f32[4]{0:T(128)S(1)} %dynamic-update-slice.9, f32[4]{0:T(128)S(1)} %dynamic-update-slice.14, ...), channel_id=1, replica_groups=mesh['tm_0'=4,'tm_1'=2,'tm_2'=2,'space_0'=2,'space_1'=4] {'space_1'}, use_global_device_ids=true, to_apply=%add.7 | all-reduce | flops 16 | bytes 128
  415.7 7.2 %fusion.38 = f32[8,2,1,32,384,3]{4,3,1,0,5,2:T(8,128)S(1)} fusion(f32[8,2,32,512,1]{3,2,1,0,4:T(8,128)S(1)} %bitcast.173, f32[2,512,384,3]{1,2,3,0:T(8,128)} %copy-done.5, f32[]{:T(128)S(6)} %div.19, f32[3]{0:T(128)S(1)} %dynamic_slice.11, f32[512,384]{0,1:T(8,128)S(1)} %broadcast_add_fusion), kind=kOutput, calls=%fused_computation.81 | convolution fusion | flops 3626827776 | bytes 8912912 | tf_op jit(solution)/shard_map/caxy,ia->cixy/dot_general | solution.py:133
  423.1 8.8 %all_to_all.62 = f32[8,2,1,32,384,3]{4,3,0,5,2,1:T(8,128)S(1)} all-to-all(f32[8,2,1,32,384,3]{4,3,0,5,2,1:T(8,128)S(1)} %copy.33), channel_id=1, replica_groups=mesh['tm_0'=4,'tm_1'=2,'tm_2'=2,'space_0'=2,'space_1'=4] {'tm_2'}, dimensions={1} | all-to-all | bytes 4718592 | tf_op jit(solution)/shard_map/all_to_all | solution.py:45
  432.0 33.8 %all_to_all.63 = f32[8,2,1,32,384,3]{4,3,1,5,2,0:T(8,128)S(1)} all-to-all(f32[8,2,1,32,384,3]{4,3,1,5,2,0:T(8,128)S(1)} %copy.34), channel_id=1, replica_groups=mesh['tm_0'=4,'tm_1'=2,'tm_2'=2,'space_0'=2,'space_1'=4] {'tm_0','tm_1'}, dimensions={0} | all-to-all | bytes 4718592 | tf_op jit(solution)/shard_map/all_to_all | solution.py:45
  466.1 7.2 %fusion.41 = f32[1,32,384,48]{2,3,1,0:T(8,128)} fusion(f32[32,384,48]{1,0,2:T(8,128)S(1)} %bitcast.183, f32[384,384]{1,0:T(8,128)S(1)} %copy-done.7), kind=kOutput, calls=%fused_computation.82 | convolution fusion | flops 2717908992 | bytes 5308416 | tf_op jit(solution)/shard_map/ctby,jb->ctjy/dot_general | solution.py:135
  473.3 7.2 %copy.37 = f32[1,32,384,48]{3,1,0,2:T(8,128)} copy(f32[1,32,384,48]{2,3,1,0:T(8,128)} %fusion.41) | data formatting | bytes 4718592 | tf_op jit(solution)/shard_map/ctby,jb->ctjy/transpose | solution.py:135
  480.5 9.5 %reshape.403 = f32[8,1,73728]{2,1,0:T(1,128)} reshape(f32[384,1,32,48]{3,2,1,0:T(8,128)} %bitcast.179) | data formatting | bytes 4718592
  504.3 19.1 %all-to-all-done.4 = f32[8,1,73728]{2,1,0:T(1,128)} async-done(((f32[8,1,73728]{2,1,0:T(1,128)}), f32[8,1,73728]{2,1,0:T(1,128)}, u32[]{:S(2)}, u32[]{:S(2)}) %all-to-all-start.4) | async-done | bytes 2359328 | tf_op jit(solution)/shard_map/all_to_all | solution.py:136
  523.5 9.3 %reduce.49 = f32[8,73728]{1,0:T(8,128)} reduce(f32[8,1,73728]{2,1,0:T(1,128)} %all-to-all-done.4, f32[]{:T(128)} %broadcast.79), dimensions={1}, to_apply=%all_to_all.53.reduce_sub_computation | reduce | bytes 4718596 | tf_op jit(solution)/shard_map/all_to_all | solution.py:136
  532.8 6.9 %reshape.404 = f32[384,1,32,48]{3,2,1,0:T(8,128)} reshape(f32[8,73728]{1,0:T(8,128)} %reduce.49) | data formatting | bytes 4718592
  539.6 9.3 %copy.53 = f32[1,32,8,48,48]{4,2,3,1,0:T(8,128)} copy(f32[1,32,8,48,48]{4,1,3,2,0:T(8,128)} %bitcast.177) | data formatting | bytes 4718592 | tf_op jit(solution)/shard_map/all_to_all | solution.py:136
  548.9 5.9 %reshape.281 = f32[32,48,384]{2,1,0:T(8,128)} reshape(f32[1,32,48,8,48]{4,3,2,1,0:T(8,128)} %bitcast.178) | data formatting | bytes 4718592 | tf_op jit(solution)/shard_map/reshape.193
  554.8 7.2 %multiply_add_fusion.3 = f32[32,48,384]{2,1,0:T(8,128)} fusion(f32[32,48,384]{2,1,0:T(8,128)S(1)} %copy-done.3, f32[32,48,384]{2,1,0:T(8,128)} %reshape.281, f32[]{:T(128)S(6)} %div.23, f32[384,384]{1,0:T(8,128)} %param.17), kind=kOutput, calls=%fused_computation.72 | convolution fusion | flops 2719088640 | bytes 7667716 | tf_op jit(solution)/shard_map/ctxa,ka->ctxk/dot_general | solution.py:137
  (130 shorter events, 97.7 us)
Async XLA Ops:
  0.6 332.8 %copy-start = (f32[512,512]{1,0:T(8,128)S(1)}, f32[512,512]{1,0:T(8,128)}, u32[]{:S(2)}) copy-start(f32[512,512]{1,0:T(8,128)} %param.16) | copy-start | bytes 3145732
  1.8 11.0 %collective-permute-start = (f32[3,48,384]{2,1,0:T(8,128)S(1)}, f32[3,48,384]{2,1,0:T(8,128)S(1)}, u32[]{:S(2)}, u32[]{:S(2)}) collective-permute-start(f32[3,48,384]{2,1,0:T(8,128)S(1)} %get-tuple-element.47), channel_id=1, source_target_pairs={{0,8},{8,16},{16,24},{24,32},{32,40},{40,48},{48,56},{56,64},{64,7... | collective-permute-start | bytes 663560 | tf_op jit(solution)/shard_map/ppermute | solution.py:21
  7.8 8.8 %collective-permute-start.1 = (f32[3,48,384]{2,1,0:T(8,128)S(1)}, f32[3,48,384]{2,1,0:T(8,128)S(1)}, u32[]{:S(2)}, u32[]{:S(2)}) collective-permute-start(f32[3,48,384]{2,1,0:T(8,128)S(1)} %get-tuple-element.46), channel_id=1, source_target_pairs={{8,0},{16,8},{24,16},{32,24},{40,32},{48,40},{56,48},{64,56},{72,6... | collective-permute-start | bytes 663560 | tf_op jit(solution)/shard_map/ppermute | solution.py:23
  12.8 8.4 %copy-start.9 = (f32[2,4,512]{2,1,0:T(4,128)S(1)}, f32[2,4,512]{2,1,0:T(4,128)}, u32[]{:S(2)}) copy-start(f32[2,4,512]{2,1,0:T(4,128)} %param.14) | copy-start | bytes 49156
  12.8 8.5 %copy-start.8 = (f32[2,4,384]{2,1,0:T(4,128)S(1)}, f32[2,4,384]{2,1,0:T(4,128)}, u32[]{:S(2)}) copy-start(f32[2,4,384]{2,1,0:T(4,128)} %param.15) | copy-start | bytes 36868
  16.7 6.2 %collective-permute-start.2 = (f32[38,3,384]{2,1,0:T(4,128)S(1)}, f32[38,3,384]{2,1,0:T(4,128)S(1)}, u32[]{:S(2)}, u32[]{:S(2)}) collective-permute-start(f32[38,3,384]{2,1,0:T(4,128)S(1)} %get-tuple-element.44), channel_id=1, source_target_pairs={{0,1},{1,2},{2,3},{3,4},{4,5},{5,6},{6,7},{8,9},{9,10},{10,11},{11... | collective-permute-start | bytes 525320 | tf_op jit(solution)/shard_map/ppermute | solution.py:21
  19.9 6.8 %collective-permute-start.3 = (f32[38,3,384]{2,1,0:T(4,128)S(1)}, f32[38,3,384]{2,1,0:T(4,128)S(1)}, u32[]{:S(2)}, u32[]{:S(2)}) collective-permute-start(f32[38,3,384]{2,1,0:T(4,128)S(1)} %get-tuple-element.45), channel_id=1, source_target_pairs={{1,0},{2,1},{3,2},{4,3},{5,4},{6,5},{7,6},{9,8},{10,9},{11,10},{12... | collective-permute-start | bytes 525320 | tf_op jit(solution)/shard_map/ppermute | solution.py:23
  59.0 12.2 %copy-start.1 = (f32[38,54,384]{2,1,0:T(8,128)S(1)}, f32[38,54,384]{2,1,0:T(8,128)}, u32[]{:S(2)}) copy-start(f32[38,54,384]{2,1,0:T(8,128)} %get-tuple-element.42) | copy-start | bytes 9455620
  59.0 12.2 %copy-start.2 = (f32[38,54,384]{2,1,0:T(8,128)S(1)}, f32[38,54,384]{2,1,0:T(8,128)}, u32[]{:S(2)}) copy-start(f32[38,54,384]{2,1,0:T(8,128)} %get-tuple-element.43) | copy-start | bytes 9455620
  77.1 18.0 %copy-start.6 = (f32[32,48,384]{2,1,0:T(8,128)S(1)}, f32[32,48,384]{2,1,0:T(8,128)}, u32[]{:S(2)}) copy-start(f32[32,48,384]{2,1,0:T(8,128)} %param.11) | copy-start | bytes 7077892
  77.1 18.0 %copy-start.7 = (f32[384,384]{1,0:T(8,128)S(1)}, f32[384,384]{1,0:T(8,128)}, u32[]{:S(2)}) copy-start(f32[384,384]{1,0:T(8,128)} %param.17) | copy-start | bytes 1769476
  93.7 1.4 copy-start.4
  261.2 13.0 %copy-start.10 = (f32[384]{0:T(512)S(1)}, f32[384]{0:T(512)}, u32[]{:S(2)}) copy-start(f32[384]{0:T(512)} %param.19) | copy-start | bytes 4612
  261.2 13.0 %copy-start.16 = (u32[128]{0:T(128)S(1)}, u32[128]{0:T(128)}, u32[]{:S(2)}) copy-start(u32[128]{0:T(128)} %constant.53) | copy-start | bytes 1540
  261.2 13.7 %copy-start.11 = (f32[512]{0:T(512)S(1)}, f32[512]{0:T(512)}, u32[]{:S(2)}) copy-start(f32[512]{0:T(512)} %param.18) | copy-start | bytes 6148
  261.2 69.5 %all-to-all-start.1 = ((f32[2,32,384,48]{2,1,0,3:T(8,128)}), f32[2,32,384,48]{2,1,0,3:T(8,128)}, u32[]{:S(2)}, u32[]{:S(2)}) async-start(f32[2,32,384,48]{2,1,0,3:T(8,128)} %copy.28), calls=%async_computation.1 | async-start | bytes 9437184 | tf_op jit(solution)/shard_map/all_to_all | solution.py:128
  341.5 2.1 copy-start.5
  343.6 6.3 %copy-start.15 = (u32[128]{0:T(128)S(1)}, u32[128]{0:T(128)}, u32[]{:S(2)}) copy-start(u32[128]{0:T(128)} %constant.58) | copy-start | bytes 1540
  343.6 21.9 %copy-start.14 = (u32[128]{0:T(128)S(1)}, u32[128]{0:T(128)}, u32[]{:S(2)}) copy-start(u32[128]{0:T(128)} %constant.63) | copy-start | bytes 1540
  343.6 35.9 %copy-start.13 = (u32[128]{0:T(128)S(1)}, u32[128]{0:T(128)}, u32[]{:S(2)}) copy-start(u32[128]{0:T(128)} %constant.68) | copy-start | bytes 1540
  343.6 50.6 %copy-start.12 = (u32[128]{0:T(128)S(1)}, u32[128]{0:T(128)}, u32[]{:S(2)}) copy-start(u32[128]{0:T(128)} %constant.73) | copy-start | bytes 1540
  490.0 8.5 %copy-start.3 = (f32[32,48,384]{2,1,0:T(8,128)S(1)}, f32[32,48,384]{2,1,0:T(8,128)}, u32[]{:S(2)}) copy-start(f32[32,48,384]{2,1,0:T(8,128)} %param.12) | copy-start | bytes 7077892
  490.0 33.5 %all-to-all-start.4 = ((f32[8,1,73728]{2,1,0:T(1,128)}), f32[8,1,73728]{2,1,0:T(1,128)}, u32[]{:S(2)}, u32[]{:S(2)}) async-start(f32[8,1,73728]{2,1,0:T(1,128)} %reshape.403), calls=%async_computation.4 | async-start | bytes 4718592 | tf_op jit(solution)/shard_map/all_to_all | solution.py:136
